TPU v7x, 256 devices: a whole 4x4x8 slice. The times are simulated.
256 devices in a mesh: block: 4 (over y), span: 8 (over z), heads: 8 (over x, core).
Axes of the slice: x: 4, y: 4, z: 8, core: 2. Of those that a mesh axis runs over, the one named last changes fastest.
Arguments:
- fresh_keys: bfloat16 [32, 16384, 8, 128], P(None, ('block', 'span'), 'heads'), may hold values from -6 to 6
- fresh_values: bfloat16 [32, 16384, 8, 128], P(None, ('block', 'span'), 'heads'), may hold values from -6 to 6
- turn_angle: float32 [16384, 64], replicated, may hold values from -3.140625 to 3.140625
Outputs:
- stored_keys: bfloat16 [32, 16384, 8, 128], P(('block', 'span'), None, 'heads')
- stored_values: bfloat16 [32, 16384, 8, 128], P(('block', 'span'), None, 'heads')
- key_scale: float32 [32, 8, 128], P(('block', 'span'), 'heads')
All inputs are finite; a program needn't handle non-finite values. Where the computation divides by a largest or mean magnitude, that divisor is 1e-20 or more.
Results may differ from a plain program's by a relative error of at most 0.001.
Values may be sent and summed in bfloat16 or wider, within the bound.
A program may use at most 192 MiB of HBM per device.

v0:
```python
import jax
import jax.numpy as jnp
from jax import lax
from jax.sharding import PartitionSpec as P


def rotate_pairs(vectors, angle):
    half = vectors.shape[-1] // 2
    cosine, sine = (jnp.cos(angle)[None, :, None, :], jnp.sin(angle)[None, :, None, :])
    first, second = (vectors[..., :half], vectors[..., half:])
    return jnp.concatenate(
        [first * cosine - second * sine, second * cosine + first * sine], axis=-1
    )


def keys_in_place(plain_keys, angle):
    wide_keys = plain_keys.astype(jnp.float32)
    return rotate_pairs(wide_keys, angle)


def local(fresh_keys, fresh_values, turn_angle):
    moved_keys, stored_values = (
        lax.all_to_all(fresh_keys, ("block", "span"), split_axis=0, concat_axis=1, tiled=True),
        lax.all_to_all(fresh_values, ("block", "span"), split_axis=0, concat_axis=1, tiled=True),
    )
    turned_keys = keys_in_place(moved_keys, turn_angle)
    key_scale = jnp.max(jnp.abs(turned_keys), axis=1)
    narrow_keys = (turned_keys / key_scale[:, None]).astype(jnp.bfloat16)
    return (narrow_keys, stored_values, key_scale)


def solution(mesh):
    return jax.shard_map(
        local,
        mesh=mesh,
        in_specs=(
            P(None, ("block", "span"), "heads", None),
            P(None, ("block", "span"), "heads", None),
            P(),
        ),
        out_specs=(
            P(("block", "span"), None, "heads", None),
            P(("block", "span"), None, "heads", None),
            P(("block", "span"), "heads", None),
        ),
        check_vma=False,
    )
```

profile of v0, /device:TPU:32, one launch (start us, length us, event | category | flops | bytes accessed | tf_op | source)
XLA Modules:
  0.0 213.3 jit_solution(15159538452021356802)
XLA Ops:
  0.6 11.4 %all-to-all-start = ((bf16[32,512,1,128]{3,1,2,0:T(8,128)(2,1)}), bf16[32,512,1,128]{3,1,2,0:T(8,128)(2,1)}, u32[]{:S(2)}, u32[]{:S(2)}) async-start(bf16[32,512,1,128]{3,1,2,0:T(8,128)(2,1)} %param.3), calls=%async_computation | async-start | bytes 8388608 | tf_op jit(solution)/shard_map/all_to_all | solution.py:23
  12.1 6.9 %copy.6 = f32[16384,64]{1,0:T(8,128)} copy(f32[16384,64]{0,1:T(8,128)} %param.5) | data formatting | bytes 8388608 | tf_op args[2]
  18.9 31.5 %fusion.2 = (f32[16384,64]{1,0:T(8,128)}, f32[16384,64]{1,0:T(8,128)}) fusion(f32[16384,64]{1,0:T(8,128)} %copy.6), kind=kLoop, calls=%fused_computation.9 | loop fusion | bytes 12582912 | tf_op jit(solution)/shard_map/cos | solution.py:9
  50.5 57.1 %all-to-all-done = bf16[32,512,1,128]{3,1,2,0:T(8,128)(2,1)} async-done(((bf16[32,512,1,128]{3,1,2,0:T(8,128)(2,1)}), bf16[32,512,1,128]{3,1,2,0:T(8,128)(2,1)}, u32[]{:S(2)}, u32[]{:S(2)}) %all-to-all-start) | async-done | bytes 4194336 | tf_op jit(solution)/shard_map/all_to_all | solution.py:23
  107.5 6.6 %all-to-all-start.1 = ((bf16[32,512,1,128]{3,1,2,0:T(8,128)(2,1)}), bf16[32,512,1,128]{3,1,2,0:T(8,128)(2,1)}, u32[]{:S(2)}, u32[]{:S(2)}) async-start(bf16[32,512,1,128]{3,1,2,0:T(8,128)(2,1)} %param.4), calls=%async_computation.1 | async-start | bytes 8388608 | tf_op jit(solution)/shard_map/all_to_all | solution.py:24
  114.1 5.1 %convert.1 = f32[1,16384,1,128]{3,1,2,0:T(8,128)} convert(bf16[1,16384,1,128]{3,1,2,0:T(8,128)(2,1)} %bitcast.2) | non-fusion elementwise | flops 2097152 | bytes 12582912 | tf_op jit(solution)/shard_map/convert_element_type | solution.py:17
  119.2 17.3 %fusion = (f32[1,16384,1,64]{3,1,2,0:T(8,128)}, f32[1,16384,1,64]{3,1,2,0:T(8,128)}) fusion(f32[16384,64]{1,0:T(8,128)} %get-tuple-element.6, f32[16384,64]{1,0:T(8,128)} %get-tuple-element.5, f32[1,16384,1,128]{3,1,2,0:T(8,128)} %convert.1), kind=kLoop, calls=%fused_computation.3 | loop fusion | flops 6291456 | bytes 25165824 | tf_op jit(solution)/shard_map/sub | solution.py:12
  136.6 0.0 copy-start
  136.6 0.0 copy-start.1
  136.6 7.7 %abs_reduce_fusion = f32[128]{0:T(128)S(1)} fusion(f32[1,16384,1,64]{3,1,2,0:T(8,128)} %get-tuple-element.4, f32[1,16384,1,64]{3,1,2,0:T(8,128)} %get-tuple-element.3), kind=kLoop, calls=%fused_computation.8 | loop fusion | flops 6291328 | bytes 8389120 | tf_op jit(solution)/shard_map/reduce_max | solution.py:27
  144.3 0.5 copy-done
  144.8 2.4 %copy-done.1 = f32[1,16384,1,64]{3,1,2,0:T(8,128)S(1)} copy-done((f32[1,16384,1,64]{3,1,2,0:T(8,128)S(1)}, f32[1,16384,1,64]{3,1,2,0:T(8,128)}, u32[]{:S(2)}) %copy-start.1) | copy-done | bytes 4194328
  147.2 0.0 copy-start.2
  147.2 3.6 %divide_convert_fusion = bf16[1,16384,1,128]{3,1,2,0:T(8,128)(2,1)} fusion(f32[128]{0:T(128)S(1)} %abs_reduce_fusion, f32[1,16384,1,64]{3,1,2,0:T(8,128)S(1)} %copy-done.1, f32[1,16384,1,64]{3,1,2,0:T(8,128)S(1)} %copy-done), kind=kLoop, calls=%fused_computation.7 | loop fusion | flops 6291456 | bytes 12583424 | tf_op jit(solution)/shard_map/convert_element_type | solution.py:28
  150.8 0.0 copy-done.2
  150.8 58.7 %all-to-all-done.1 = bf16[32,512,1,128]{3,1,2,0:T(8,128)(2,1)} async-done(((bf16[32,512,1,128]{3,1,2,0:T(8,128)(2,1)}), bf16[32,512,1,128]{3,1,2,0:T(8,128)(2,1)}, u32[]{:S(2)}, u32[]{:S(2)}) %all-to-all-start.1) | async-done | bytes 4194336 | tf_op jit(solution)/shard_map/all_to_all | solution.py:24
  209.6 3.7 %copy.9 = bf16[1,16384,1,128]{3,1,2,0:T(8,128)(2,1)} copy(bf16[1,16384,1,128]{3,1,2,0:T(8,128)(2,1)} %bitcast.4) | data formatting | bytes 8388608
Async XLA Ops:
  0.6 106.9 %all-to-all-start = ((bf16[32,512,1,128]{3,1,2,0:T(8,128)(2,1)}), bf16[32,512,1,128]{3,1,2,0:T(8,128)(2,1)}, u32[]{:S(2)}, u32[]{:S(2)}) async-start(bf16[32,512,1,128]{3,1,2,0:T(8,128)(2,1)} %param.3), calls=%async_computation | async-start | bytes 8388608 | tf_op jit(solution)/shard_map/all_to_all | solution.py:23
  107.5 102.1 %all-to-all-start.1 = ((bf16[32,512,1,128]{3,1,2,0:T(8,128)(2,1)}), bf16[32,512,1,128]{3,1,2,0:T(8,128)(2,1)}, u32[]{:S(2)}, u32[]{:S(2)}) async-start(bf16[32,512,1,128]{3,1,2,0:T(8,128)(2,1)} %param.4), calls=%async_computation.1 | async-start | bytes 8388608 | tf_op jit(solution)/shard_map/all_to_all | solution.py:24
  136.6 8.2 %copy-start = (f32[1,16384,1,64]{3,1,2,0:T(8,128)S(1)}, f32[1,16384,1,64]{3,1,2,0:T(8,128)}, u32[]{:S(2)}) copy-start(f32[1,16384,1,64]{3,1,2,0:T(8,128)} %get-tuple-element.3) | copy-start | bytes 12582916
  136.6 10.6 %copy-start.1 = (f32[1,16384,1,64]{3,1,2,0:T(8,128)S(1)}, f32[1,16384,1,64]{3,1,2,0:T(8,128)}, u32[]{:S(2)}) copy-start(f32[1,16384,1,64]{3,1,2,0:T(8,128)} %get-tuple-element.4) | copy-start | bytes 12582916
  147.2 3.6 %copy-start.2 = (f32[128]{0:T(128)}, f32[128]{0:T(128)S(1)}, u32[]{:S(2)}) copy-start(f32[128]{0:T(128)S(1)} %abs_reduce_fusion) | copy-start | bytes 1540
where the time goes:
time: 215 us; the launch traced here: 213 us
  waiting for transfers between devices  116 us (54%)
  local copies, waits for them, and re-layouts  45 us (21%)
  other arithmetic  33.8 us (16%)
  starting transfers between devices  18 us (8%)
    all_to_all x1, waiting for transfers between devices, local(): lax.all_to_all(fresh_values, ('block', 'span'), split_axis=0, concat_axis...  58.7 us
    all_to_all x1, waiting for transfers between devices, local(): lax.all_to_all(fresh_keys, ('block', 'span'), split_axis=0, concat_axis=1...  57.1 us
    cos x1, local copies, waits for them, and re-layouts, rotate_pairs(): jnp.cos(angle)[None, :, None, :]  31.5 us
    sub x1, other arithmetic, rotate_pairs(): first * cosine - second * sine  17.3 us
    unnamed x8, local copies, waits for them, and re-layouts  13.5 us
    all_to_all x1, starting transfers between devices, local(): lax.all_to_all(fresh_keys, ('block', 'span'), split_axis=0, concat_axis=1...  11.4 us
    reduce_max x1, other arithmetic, local(): key_scale = jnp.max(jnp.abs(turned_keys), axis=1)  7.69 us
    all_to_all x1, starting transfers between devices, local(): lax.all_to_all(fresh_values, ('block', 'span'), split_axis=0, concat_axis...  6.62 us
  transfers between devices with their start and end apart: 2, of which 2 were waited for; matrix products, arithmetic and copies ran while one was open for 34% of the time, Pallas kernels for 0%

commit v1 on v0

v1 whole, which is shorter than its diff:
```python
import functools

import jax
import jax.numpy as jnp
from jax import lax
from jax.experimental import pallas as pl
from jax.experimental.pallas import tpu as pltpu
from jax.sharding import PartitionSpec as P

MESH = pl.DeviceIdType.MESH
DISTANCES = (4, 1, 2, 3)


def kernel(
    blocks, spans, rows,
    keys_ref, values_ref, angle_ref,
    out_keys, out_values, scale_ref,
    got_keys, angle, table, send_sem, recv_sem, own_sem,
):
    y, z, h = lax.axis_index("block"), lax.axis_index("span"), lax.axis_index("heads")
    core = lax.rem(h, 2)
    me = y * spans + z
    length = angle.shape[1]
    half = angle.shape[0]

    barrier = pltpu.get_barrier_semaphore()
    for step in range(1, blocks * spans):
        there = (lax.rem(y + step // spans, blocks), lax.rem(z + step % spans, spans), h)
        pl.semaphore_signal(barrier, inc=1, device_id=there, device_id_type=MESH)
    pl.semaphore_wait(barrier, blocks * spans - 1)

    def part(ref, index):
        return ref.at[pl.ds(pl.multiple_of(index * rows, rows), rows)]

    def copy(which, dy, dz):
        source, target = ((keys_ref, got_keys), (values_ref, out_values))[which]
        ty, tz = lax.rem(y + dy, blocks), lax.rem(z + dz + spans, spans)
        slot = which * blocks * spans + (dz % spans) * blocks + dy
        return pltpu.make_async_remote_copy(
            src_ref=part(source, ty * spans + tz),
            dst_ref=part(target, me),
            send_sem=send_sem.at[slot],
            recv_sem=recv_sem.at[slot],
            device_id=(ty, tz, h),
            device_id_type=MESH,
        )

    def arrival(which, dy, dz):
        source, target = ((keys_ref, got_keys), (values_ref, out_values))[which]
        fy, fz = lax.rem(y - dy + blocks, blocks), lax.rem(z - dz + spans, spans)
        slot = which * blocks * spans + dz * blocks + dy
        return pltpu.make_async_remote_copy(
            src_ref=part(source, me),
            dst_ref=part(target, fy * spans + fz),
            send_sem=send_sem.at[slot],
            recv_sem=recv_sem.at[slot],
            device_id=(fy, fz, h),
            device_id_type=MESH,
        )

    angle_copy = pltpu.make_async_copy(angle_ref, angle, own_sem.at[0])
    angle_copy.start()
    for which in range(2):
        for dy in (1, 3, 2):
            copy(which, dy, 0).start()
        for turn in range(blocks):
            for place, distance in enumerate(DISTANCES):
                for side, dz in enumerate((distance, -distance)):
                    if side and 2 * distance == spans:
                        continue
                    copy(which, lax.rem(2 * core + (turn + place + side), blocks), dz).start()
    own_keys = pltpu.make_async_copy(part(keys_ref, me), part(got_keys, me), own_sem.at[1])
    own_values = pltpu.make_async_copy(part(values_ref, me), part(out_values, me), own_sem.at[2])
    own_keys.start()
    own_values.start()
    angle_copy.wait()

    def fill(index, carry):
        start = pl.multiple_of(index * 128, 128)
        here = angle[:, pl.ds(start, 128)]
        both = jnp.concatenate([jnp.cos(here), jnp.sin(here)], axis=0)
        table[pl.ds(start, 128), :] = both.T
        return carry

    lax.fori_loop(0, length // 128, fill, 0)

    own_keys.wait()
    for slot in range(1, blocks * spans):
        arrival(0, slot % blocks, slot // blocks).wait_recv()

    first = lax.broadcasted_iota(jnp.int32, (128, 2 * half), 1) < half

    def turn_rows(index, most):
        at = pl.ds(pl.multiple_of(index * 128, 128), 128)
        wide = got_keys[at, :].astype(jnp.float32)
        here = table[at, :]
        swapped = pltpu.roll(here, half, 1)
        cosine = jnp.where(first, here, swapped)
        sine = jnp.where(first, -swapped, here)
        turned = wide * cosine + pltpu.roll(wide, half, 1) * sine
        table[at, :] = turned
        return jnp.maximum(most, jnp.max(jnp.abs(turned).reshape(16, 8, 2 * half), axis=0))

    most = lax.fori_loop(0, length // 128, turn_rows, jnp.zeros((8, 2 * half), jnp.float32))
    scale = jnp.max(most, axis=0, keepdims=True)
    scale_ref[...] = scale
    factor = 1.0 / scale

    def narrow_rows(index, carry):
        at = pl.ds(pl.multiple_of(index * 128, 128), 128)
        out_keys[at, :] = (table[at, :] * factor).astype(jnp.bfloat16)
        return carry

    lax.fori_loop(0, length // 128, narrow_rows, 0)

    own_values.wait()
    for slot in range(1, blocks * spans):
        arrival(1, slot % blocks, slot // blocks).wait_recv()
    for which in range(2):
        for slot in range(1, blocks * spans):
            arrival(which, slot % blocks, slot // blocks).wait_send()


def local(blocks, spans, fresh_keys, fresh_values, turn_angle):
    batch, rows, _, size = fresh_keys.shape
    length = batch * rows
    keys, values, scale = pl.pallas_call(
        functools.partial(kernel, blocks, spans, rows),
        out_shape=[
            jax.ShapeDtypeStruct((length, size), jnp.bfloat16),
            jax.ShapeDtypeStruct((length, size), jnp.bfloat16),
            jax.ShapeDtypeStruct((1, size), jnp.float32),
        ],
        in_specs=[pl.BlockSpec(memory_space=pltpu.HBM)] * 3,
        out_specs=[
            pl.BlockSpec(memory_space=pltpu.VMEM),
            pl.BlockSpec(memory_space=pl.ANY),
            pl.BlockSpec(memory_space=pltpu.VMEM),
        ],
        scratch_shapes=[
            pltpu.VMEM((length, size), jnp.bfloat16),
            pltpu.VMEM((size // 2, length), jnp.float32),
            pltpu.VMEM((length, size), jnp.float32),
            pltpu.SemaphoreType.DMA((2 * batch,)),
            pltpu.SemaphoreType.DMA((2 * batch,)),
            pltpu.SemaphoreType.DMA((3,)),
        ],
        compiler_params=pltpu.CompilerParams(
            collective_id=0, has_side_effects=True, vmem_limit_bytes=32 << 20
        ),
    )(
        *(
            pltpu.with_memory_space_constraint(array, pltpu.HBM)
            for array in (
                fresh_keys.reshape(length, size),
                fresh_values.reshape(length, size),
                turn_angle.T,
            )
        )
    )
    return (
        keys.reshape(1, length, 1, size),
        values.reshape(1, length, 1, size),
        scale.reshape(1, 1, size),
    )


def solution(mesh):
    blocks, spans = mesh.shape["block"], mesh.shape["span"]
    return jax.shard_map(
        functools.partial(local, blocks, spans),
        mesh=mesh,
        in_specs=(
            P(None, ("block", "span"), "heads", None),
            P(None, ("block", "span"), "heads", None),
            P(),
        ),
        out_specs=(
            P(("block", "span"), None, "heads", None),
            P(("block", "span"), None, "heads", None),
            P(("block", "span"), "heads", None),
        ),
        check_vma=False,
    )
```

time: 215 us -> 198 us (0.921)
  Pallas kernels: 0 us -> 193 us
  waiting for transfers between devices: 116 us -> 0 us
  local copies, waits for them, and re-layouts: 45 us -> 4.54 us
  other arithmetic: 33.8 us -> 0 us
  starting transfers between devices: 18 us -> 0 us
    pallas_call x0 -> x1, Pallas kernels: none -> 193 us  [local(): pl.pallas_call(functools.partial(kernel, blocks, spans, rows), out_shape=...]
    all_to_all x2 -> x0, waiting for transfers between devices: 116 us -> none  [the longest x1 58.7 us: local(): lax.all_to_all(fresh_values, ('block', 'span'), split_axis=0, concat_axis...]
    cos x1 -> x0, local copies, waits for them, and re-layouts: 31.5 us -> none  [rotate_pairs(): jnp.cos(angle)[None, :, None, :]]
    all_to_all x2 -> x0, starting transfers between devices: 18 us -> none  [the longest x1 11.4 us: local(): lax.all_to_all(fresh_keys, ('block', 'span'), split_axis=0, concat_axis=1...]
    sub x1 -> x0, other arithmetic: 17.3 us -> none  [rotate_pairs(): first * cosine - second * sine]
    unnamed x8 -> x3, local copies, waits for them, and re-layouts: 13.5 us -> 4.54 us
    convert_element_type x2 -> x0, other arithmetic: 8.73 us -> none  [the longest x1 5.1 us: keys_in_place(): wide_keys = plain_keys.astype(jnp.float32)]
    reduce_max x1 -> x0, other arithmetic: 7.69 us -> none  [local(): key_scale = jnp.max(jnp.abs(turned_keys), axis=1)]
  transfers between devices with their start and end apart: 2 -> 0, of which waited for: 2 -> 0; matrix products, arithmetic and copies ran while one was open for 34% -> 0% of each run, Pallas kernels for 0% -> 0%
where the time goes in v1:
time: 198 us
  Pallas kernels  193 us (97%)
  local copies, waits for them, and re-layouts  4.54 us (2%)
    pallas_call x1, Pallas kernels, local(): pl.pallas_call(functools.partial(kernel, blocks, spans, rows), out_shape=...  193 us
    unnamed x3, local copies, waits for them, and re-layouts  4.54 us

profile of v1, /device:TPU:32, one launch (start us, length us, event | category | flops | bytes accessed | tf_op | source)
XLA Modules:
  0.0 198.0 jit_solution(2907059962906197478)
XLA Ops:
  0.6 192.8 %shard_map.58 = (bf16[16384,128]{1,0:T(8,128)(2,1)S(1)}, bf16[16384,128]{1,0:T(8,128)(2,1)S(1)}, f32[1,128]{1,0:T(1,128)S(1)}) custom-call(bf16[16384,128]{1,0:T(8,128)(2,1)} %bitcast.9, bf16[16384,128]{1,0:T(8,128)(2,1)} %bitcast.10, f32[64,16384]{1,0:T(8,128)} %bitcast.11), custom_call_target="tpu_custom_call" | custom-call | tf_op jit(solution)/shard_map/pallas_call | solution.py:127
  193.4 2.0 %copy.9 = bf16[1,16384,1,128]{3,1,2,0:T(8,128)(2,1)} copy(bf16[1,16384,1,128]{3,1,2,0:T(8,128)(2,1)S(1)} %bitcast.7) | data formatting | bytes 8388608
  195.5 2.0 %copy.10 = bf16[1,16384,1,128]{3,1,2,0:T(8,128)(2,1)} copy(bf16[1,16384,1,128]{3,1,2,0:T(8,128)(2,1)S(1)} %bitcast.6) | data formatting | bytes 8388608
  197.5 0.5 copy.11

commit v2 on v1

v2 whole, which is shorter than its diff:
```python
import functools

import jax
import jax.numpy as jnp
from jax import lax
from jax.experimental import pallas as pl
from jax.experimental.pallas import tpu as pltpu
from jax.sharding import PartitionSpec as P

MESH = pl.DeviceIdType.MESH
DISTANCES = (4, 1, 2, 3)


def kernel(
    blocks, spans, rows,
    keys_ref, values_ref, angle_ref,
    out_keys, out_values, scale_ref,
    keys, values, got_keys, angle, table, send_sem, recv_sem, own_sem,
):
    y, z, h = lax.axis_index("block"), lax.axis_index("span"), lax.axis_index("heads")
    core = lax.rem(h, 2)
    me = y * spans + z
    length = angle.shape[1]
    half = angle.shape[0]

    barrier = pltpu.get_barrier_semaphore()
    for step in range(1, blocks * spans):
        there = (lax.rem(y + step // spans, blocks), lax.rem(z + step % spans, spans), h)
        pl.semaphore_signal(barrier, inc=1, device_id=there, device_id_type=MESH)
    keys_in = pltpu.make_async_copy(keys_ref, keys, own_sem.at[0])
    values_in = pltpu.make_async_copy(values_ref, values, own_sem.at[1])
    angle_in = pltpu.make_async_copy(angle_ref, angle, own_sem.at[2])
    keys_in.start()
    values_in.start()
    pl.semaphore_wait(barrier, blocks * spans - 1)

    def part(ref, index):
        return ref.at[pl.ds(pl.multiple_of(index * rows, rows), rows)]

    def send(which, dy, dz):
        source, target = ((keys, got_keys), (values, out_values))[which]
        ty, tz = lax.rem(y + dy, blocks), lax.rem(z + dz + spans, spans)
        pltpu.make_async_remote_copy(
            src_ref=part(source, ty * spans + tz),
            dst_ref=part(target, me),
            send_sem=send_sem.at[which],
            recv_sem=recv_sem.at[which],
            device_id=(ty, tz, h),
            device_id_type=MESH,
        ).start()

    def others(which):
        source, target = ((keys, got_keys), (values, out_values))[which]
        count = (blocks * spans - 1) * rows
        return pltpu.make_async_remote_copy(
            src_ref=source.at[pl.ds(0, count)],
            dst_ref=target.at[pl.ds(0, count)],
            send_sem=send_sem.at[which],
            recv_sem=recv_sem.at[which],
            device_id=(lax.rem(y + 1, blocks), z, h),
            device_id_type=MESH,
        )

    for which, staged in enumerate((keys_in, values_in)):
        staged.wait()
        for turn in range(blocks):
            for place, distance in enumerate(DISTANCES):
                for side, dz in enumerate((distance, -distance)):
                    if side and 2 * distance == spans:
                        continue
                    send(which, lax.rem(2 * core + (turn + place + side), blocks), dz)
            if turn:
                send(which, turn, 0)
    own_keys = pltpu.make_async_copy(part(keys_ref, me), part(got_keys, me), own_sem.at[0])
    own_values = pltpu.make_async_copy(part(values_ref, me), part(out_values, me), own_sem.at[1])
    angle_in.start()
    own_keys.start()
    own_values.start()
    angle_in.wait()

    def fill(index, carry):
        start = pl.multiple_of(index * 128, 128)
        here = angle[:, pl.ds(start, 128)]
        both = jnp.concatenate([jnp.cos(here), jnp.sin(here)], axis=0)
        table[pl.ds(start, 128), :] = both.T
        return carry

    lax.fori_loop(0, length // 128, fill, 0)

    own_keys.wait()
    others(0).wait_recv()

    first = lax.broadcasted_iota(jnp.int32, (128, 2 * half), 1) < half

    def turn_rows(index, most):
        at = pl.ds(pl.multiple_of(index * 128, 128), 128)
        wide = got_keys[at, :].astype(jnp.float32)
        here = table[at, :]
        swapped = pltpu.roll(here, half, 1)
        cosine = jnp.where(first, here, swapped)
        sine = jnp.where(first, -swapped, here)
        turned = wide * cosine + pltpu.roll(wide, half, 1) * sine
        table[at, :] = turned
        return jnp.maximum(most, jnp.max(jnp.abs(turned).reshape(16, 8, 2 * half), axis=0))

    most = lax.fori_loop(0, length // 128, turn_rows, jnp.zeros((8, 2 * half), jnp.float32))
    scale = jnp.max(most, axis=0, keepdims=True)
    scale_ref[...] = scale
    factor = 1.0 / scale

    def narrow_rows(index, carry):
        at = pl.ds(pl.multiple_of(index * 128, 128), 128)
        out_keys[at, :] = (table[at, :] * factor).astype(jnp.bfloat16)
        return carry

    lax.fori_loop(0, length // 128, narrow_rows, 0)

    own_values.wait()
    others(0).wait_send()
    others(1).wait_send()
    others(1).wait_recv()


def put_out(keys, values, scale, out_keys, out_values, out_scale, sem):
    copies = [pltpu.make_async_copy(scale, out_scale, sem.at[0])]
    half = keys.shape[0] // 2
    for index, (source, target) in enumerate(((keys, out_keys), (values, out_values))):
        for piece in range(2):
            at = pl.ds(piece * half, half)
            copies.append(
                pltpu.make_async_copy(source.at[at], target.at[at], sem.at[1 + 2 * index + piece])
            )
    for one in copies:
        one.start()
    for one in copies:
        one.wait()


def local(blocks, spans, fresh_keys, fresh_values, turn_angle):
    batch, rows, _, size = fresh_keys.shape
    length = batch * rows
    shapes = [
        jax.ShapeDtypeStruct((length, size), jnp.bfloat16),
        jax.ShapeDtypeStruct((length, size), jnp.bfloat16),
        jax.ShapeDtypeStruct((1, size), jnp.float32),
    ]
    results = pl.pallas_call(
        functools.partial(kernel, blocks, spans, rows),
        out_shape=shapes,
        in_specs=[pl.BlockSpec(memory_space=pltpu.HBM)] * 3,
        out_specs=[
            pl.BlockSpec(memory_space=pltpu.VMEM),
            pl.BlockSpec(memory_space=pl.ANY),
            pl.BlockSpec(memory_space=pltpu.VMEM),
        ],
        scratch_shapes=[
            pltpu.VMEM((length, size), jnp.bfloat16),
            pltpu.VMEM((length, size), jnp.bfloat16),
            pltpu.VMEM((length, size), jnp.bfloat16),
            pltpu.VMEM((size // 2, length), jnp.float32),
            pltpu.VMEM((length, size), jnp.float32),
            pltpu.SemaphoreType.DMA((2,)),
            pltpu.SemaphoreType.DMA((2,)),
            pltpu.SemaphoreType.DMA((3,)),
        ],
        compiler_params=pltpu.CompilerParams(
            collective_id=0, has_side_effects=True, vmem_limit_bytes=40 << 20
        ),
    )(
        *(
            pltpu.with_memory_space_constraint(array, pltpu.HBM)
            for array in (
                fresh_keys.reshape(length, size),
                fresh_values.reshape(length, size),
                turn_angle.T,
            )
        )
    )
    keys, values, scale = pl.pallas_call(
        put_out,
        out_shape=shapes,
        in_specs=[pl.BlockSpec(memory_space=pl.ANY)] * 3,
        out_specs=[pl.BlockSpec(memory_space=pl.ANY)] * 3,
        scratch_shapes=[pltpu.SemaphoreType.DMA((5,))],
        compiler_params=pltpu.CompilerParams(vmem_limit_bytes=1 << 20),
    )(*results)
    return (
        keys.reshape(1, length, 1, size),
        values.reshape(1, length, 1, size),
        scale.reshape(1, 1, size),
    )


def solution(mesh):
    blocks, spans = mesh.shape["block"], mesh.shape["span"]
    return jax.shard_map(
        functools.partial(local, blocks, spans),
        mesh=mesh,
        in_specs=(
            P(None, ("block", "span"), "heads", None),
            P(None, ("block", "span"), "heads", None),
            P(),
        ),
        out_specs=(
            P(("block", "span"), None, "heads", None),
            P(("block", "span"), None, "heads", None),
            P(("block", "span"), "heads", None),
        ),
        check_vma=False,
    )
```

time: 198 us -> 196 us (0.990)
  local copies, waits for them, and re-layouts: 4.54 us -> 0 us
  Pallas kernels: 193 us -> 195 us
    unnamed x3 -> x0, local copies, waits for them, and re-layouts: 4.54 us -> none
    pallas_call x0 -> x1, Pallas kernels: none -> 3.38 us  [local(): pl.pallas_call(put_out, out_shape=shapes, in_specs=[pl.BlockSpec(memory_s...]
where the time goes in v2:
time: 196 us
  Pallas kernels  195 us (99%)
    pallas_call x1, Pallas kernels, local(): pl.pallas_call(functools.partial(kernel, blocks, spans, rows), out_shape=...  192 us

profile of v2, /device:TPU:32, one launch (start us, length us, event | category | flops | bytes accessed | tf_op | source)
XLA Modules:
  0.0 195.7 jit_solution(12078678219072098660)
XLA Ops:
  0.6 191.6 %shard_map.58 = (bf16[16384,128]{1,0:T(8,128)(2,1)S(1)}, bf16[16384,128]{1,0:T(8,128)(2,1)S(1)}, f32[1,128]{1,0:T(1,128)S(1)}) custom-call(bf16[16384,128]{1,0:T(8,128)(2,1)} %bitcast.6, bf16[16384,128]{1,0:T(8,128)(2,1)} %bitcast.7, f32[64,16384]{1,0:T(8,128)} %bitcast.8), custom_call_target="tpu_custom_call" | custom-call | tf_op jit(solution)/shard_map/pallas_call | solution.py:147
  192.3 3.4 %shard_map.59 = (bf16[16384,128]{1,0:T(8,128)(2,1)}, bf16[16384,128]{1,0:T(8,128)(2,1)}, f32[1,128]{1,0:T(1,128)}) custom-call(bf16[16384,128]{1,0:T(8,128)(2,1)S(1)} %get-tuple-element.9.keys, bf16[16384,128]{1,0:T(8,128)(2,1)S(1)} %get-tuple-element.10.values, f32[1,128]{1,0:T(1,128)S(1)} %get-tuple-element.11.scale), custom_call_target="tpu_custom_call" | custom-call | tf_op jit(solution)/shard_map/pallas_call | solution.py:179

commit v3 on v2

--- a/solution.py
+++ b/solution.py
@@ -8,14 +8,15 @@
 from jax.sharding import PartitionSpec as P
 
 MESH = pl.DeviceIdType.MESH
-DISTANCES = (4, 1, 2, 3)
+DISTANCES = (4, 3, 2, 1)
+AHEAD = ((1, 2, 3, 4), (1,))
 
 
 def kernel(
     blocks, spans, rows,
     keys_ref, values_ref, angle_ref,
     out_keys, out_values, scale_ref,
-    keys, values, got_keys, angle, table, send_sem, recv_sem, own_sem,
+    got_keys, angle, table, send_sem, recv_sem, own_sem, span_up, span_down, block_up, block_down,
 ):
     y, z, h = lax.axis_index("block"), lax.axis_index("span"), lax.axis_index("heads")
     core = lax.rem(h, 2)
@@ -23,22 +24,11 @@
     length = angle.shape[1]
     half = angle.shape[0]
 
-    barrier = pltpu.get_barrier_semaphore()
-    for step in range(1, blocks * spans):
-        there = (lax.rem(y + step // spans, blocks), lax.rem(z + step % spans, spans), h)
-        pl.semaphore_signal(barrier, inc=1, device_id=there, device_id_type=MESH)
-    keys_in = pltpu.make_async_copy(keys_ref, keys, own_sem.at[0])
-    values_in = pltpu.make_async_copy(values_ref, values, own_sem.at[1])
-    angle_in = pltpu.make_async_copy(angle_ref, angle, own_sem.at[2])
-    keys_in.start()
-    values_in.start()
-    pl.semaphore_wait(barrier, blocks * spans - 1)
-
     def part(ref, index):
         return ref.at[pl.ds(pl.multiple_of(index * rows, rows), rows)]
 
     def send(which, dy, dz):
-        source, target = ((keys, got_keys), (values, out_values))[which]
+        source, target = ((keys_ref, got_keys), (values_ref, out_values))[which]
         ty, tz = lax.rem(y + dy, blocks), lax.rem(z + dz + spans, spans)
         pltpu.make_async_remote_copy(
             src_ref=part(source, ty * spans + tz),
@@ -50,7 +40,7 @@
         ).start()
 
     def others(which):
-        source, target = ((keys, got_keys), (values, out_values))[which]
+        source, target = ((keys_ref, got_keys), (values_ref, out_values))[which]
         count = (blocks * spans - 1) * rows
         return pltpu.make_async_remote_copy(
             src_ref=source.at[pl.ds(0, count)],
@@ -61,19 +51,52 @@
             device_id_type=MESH,
         )
 
-    for which, staged in enumerate((keys_in, values_in)):
-        staged.wait()
+    def sides(distance):
+        return (distance,) if 2 * distance == spans else (distance, -distance)
+
+    def send_in_ring(which, distance):
+        if distance in AHEAD[which]:
+            for dz in sides(distance):
+                send(which, 0, dz)
+
+    angle_in = pltpu.make_async_copy(angle_ref, angle, own_sem.at[2])
+    angle_in.start()
+
+    span_next, span_last = (y, lax.rem(z + 1, spans), h), (y, lax.rem(z + spans - 1, spans), h)
+    block_next, block_last = (lax.rem(y + 1, blocks), z, h), (lax.rem(y + blocks - 1, blocks), z, h)
+    barrier = pltpu.get_barrier_semaphore()
+    for neighbour in (span_next, span_last, block_next, block_last):
+        pl.semaphore_signal(barrier, inc=1, device_id=neighbour, device_id_type=MESH)
+    pl.semaphore_wait(barrier, 4)
+
+    def pass_on(up, following, down, before):
+        pl.semaphore_signal(up, inc=1, device_id=following, device_id_type=MESH)
+        pl.semaphore_signal(down, inc=1, device_id=before, device_id_type=MESH)
+        pl.semaphore_wait(up, 1)
+        pl.semaphore_wait(down, 1)
+
+    for which in range(2):
+        send_in_ring(which, 1)
+    for distance in range(2, spans // 2 + 1):
+        pass_on(span_up, span_next, span_down, span_last)
+        for which in range(2):
+            send_in_ring(which, distance)
+    for _ in range(blocks // 2):
+        pass_on(block_up, block_next, block_down, block_last)
+
+    for which in range(2):
         for turn in range(blocks):
             for place, distance in enumerate(DISTANCES):
-                for side, dz in enumerate((distance, -distance)):
-                    if side and 2 * distance == spans:
-                        continue
-                    send(which, lax.rem(2 * core + (turn + place + side), blocks), dz)
+                for side, dz in enumerate(sides(distance)):
+                    step = 2 * core + (turn + place + side)
+                    if distance not in AHEAD[which]:
+                        send(which, lax.rem(step, blocks), dz)
+                    elif turn < blocks - 1:
+                        send(which, lax.rem(step, blocks - 1) + 1, dz)
             if turn:
-                send(which, turn, 0)
+                send(which, (1, 3, 2)[turn - 1], 0)
     own_keys = pltpu.make_async_copy(part(keys_ref, me), part(got_keys, me), own_sem.at[0])
     own_values = pltpu.make_async_copy(part(values_ref, me), part(out_values, me), own_sem.at[1])
-    angle_in.start()
     own_keys.start()
     own_values.start()
     angle_in.wait()
@@ -155,16 +178,15 @@
         ],
         scratch_shapes=[
             pltpu.VMEM((length, size), jnp.bfloat16),
-            pltpu.VMEM((length, size), jnp.bfloat16),
-            pltpu.VMEM((length, size), jnp.bfloat16),
             pltpu.VMEM((size // 2, length), jnp.float32),
             pltpu.VMEM((length, size), jnp.float32),
             pltpu.SemaphoreType.DMA((2,)),
             pltpu.SemaphoreType.DMA((2,)),
             pltpu.SemaphoreType.DMA((3,)),
+            *[pltpu.SemaphoreType.REGULAR] * 4,
         ],
         compiler_params=pltpu.CompilerParams(
-            collective_id=0, has_side_effects=True, vmem_limit_bytes=40 << 20
+            collective_id=0, has_side_effects=True, vmem_limit_bytes=32 << 20
         ),
     )(
         *(

time: 196 us -> 194 us (0.990)
  no operation moved by 1% of the time
where the time goes in v3:
time: 194 us
  Pallas kernels  194 us (100%)
    pallas_call x1, Pallas kernels, local(): pl.pallas_call(functools.partial(kernel, blocks, spans, rows), out_shape=...  190 us

profile of v3, /device:TPU:32, one launch (start us, length us, event | category | flops | bytes accessed | tf_op | source)
XLA Modules:
  0.0 194.2 jit_solution(17639570125878104204)
XLA Ops:
  0.6 190.1 %shard_map.58 = (bf16[16384,128]{1,0:T(8,128)(2,1)S(1)}, bf16[16384,128]{1,0:T(8,128)(2,1)S(1)}, f32[1,128]{1,0:T(1,128)S(1)}) custom-call(bf16[16384,128]{1,0:T(8,128)(2,1)} %bitcast.6, bf16[16384,128]{1,0:T(8,128)(2,1)} %bitcast.7, f32[64,16384]{1,0:T(8,128)} %bitcast.8), custom_call_target="tpu_custom_call" | custom-call | tf_op jit(solution)/shard_map/pallas_call | solution.py:170
  190.8 3.4 %shard_map.59 = (bf16[16384,128]{1,0:T(8,128)(2,1)}, bf16[16384,128]{1,0:T(8,128)(2,1)}, f32[1,128]{1,0:T(1,128)}) custom-call(bf16[16384,128]{1,0:T(8,128)(2,1)S(1)} %get-tuple-element.9.keys, bf16[16384,128]{1,0:T(8,128)(2,1)S(1)} %get-tuple-element.10.values, f32[1,128]{1,0:T(1,128)S(1)} %get-tuple-element.11.scale), custom_call_target="tpu_custom_call" | custom-call | tf_op jit(solution)/shard_map/pallas_call | solution.py:201

commit v4 on v3

--- a/solution.py
+++ b/solution.py
@@ -8,7 +8,7 @@
 from jax.sharding import PartitionSpec as P
 
 MESH = pl.DeviceIdType.MESH
-DISTANCES = (4, 3, 2, 1)
+DISTANCES = (3, 4, 2, 1)
 AHEAD = ((1, 2, 3, 4), (1,))
 
 

time: 194 us -> 194 us (level)
  no operation moved by 1% of the time
where the time goes in v4:
time: 194 us
  Pallas kernels  193 us (99%)
    pallas_call x1, Pallas kernels, local(): pl.pallas_call(functools.partial(kernel, blocks, spans, rows), out_shape=...  189 us

profile of v4, /device:TPU:32, one launch (start us, length us, event | category | flops | bytes accessed | tf_op | source)
XLA Modules:
  0.0 193.5 jit_solution(11087301401813096932)
XLA Ops:
  0.6 189.5 %shard_map.58 = (bf16[16384,128]{1,0:T(8,128)(2,1)S(1)}, bf16[16384,128]{1,0:T(8,128)(2,1)S(1)}, f32[1,128]{1,0:T(1,128)S(1)}) custom-call(bf16[16384,128]{1,0:T(8,128)(2,1)} %bitcast.6, bf16[16384,128]{1,0:T(8,128)(2,1)} %bitcast.7, f32[64,16384]{1,0:T(8,128)} %bitcast.8), custom_call_target="tpu_custom_call" | custom-call | tf_op jit(solution)/shard_map/pallas_call | solution.py:170
  190.1 3.4 %shard_map.59 = (bf16[16384,128]{1,0:T(8,128)(2,1)}, bf16[16384,128]{1,0:T(8,128)(2,1)}, f32[1,128]{1,0:T(1,128)}) custom-call(bf16[16384,128]{1,0:T(8,128)(2,1)S(1)} %get-tuple-element.9.keys, bf16[16384,128]{1,0:T(8,128)(2,1)S(1)} %get-tuple-element.10.values, f32[1,128]{1,0:T(1,128)S(1)} %get-tuple-element.11.scale), custom_call_target="tpu_custom_call" | custom-call | tf_op jit(solution)/shard_map/pallas_call | solution.py:201

commit v5 on v4

--- a/solution.py
+++ b/solution.py
@@ -16,7 +16,7 @@
     blocks, spans, rows,
     keys_ref, values_ref, angle_ref,
     out_keys, out_values, scale_ref,
-    got_keys, angle, table, send_sem, recv_sem, own_sem, span_up, span_down, block_up, block_down,
+    got_keys, angle, table, send_sem, recv_sem, own_sem, near, far, across,
 ):
     y, z, h = lax.axis_index("block"), lax.axis_index("span"), lax.axis_index("heads")
     core = lax.rem(h, 2)
@@ -69,20 +69,22 @@
         pl.semaphore_signal(barrier, inc=1, device_id=neighbour, device_id_type=MESH)
     pl.semaphore_wait(barrier, 4)
 
-    def pass_on(up, following, down, before):
-        pl.semaphore_signal(up, inc=1, device_id=following, device_id_type=MESH)
-        pl.semaphore_signal(down, inc=1, device_id=before, device_id_type=MESH)
-        pl.semaphore_wait(up, 1)
-        pl.semaphore_wait(down, 1)
+    def pass_on(sems, devices):
+        for index, device in enumerate(devices):
+            pl.semaphore_signal(sems.at[index], inc=1, device_id=device, device_id_type=MESH)
+        for index in range(len(devices)):
+            pl.semaphore_wait(sems.at[index], 1)
 
     for which in range(2):
         send_in_ring(which, 1)
-    for distance in range(2, spans // 2 + 1):
-        pass_on(span_up, span_next, span_down, span_last)
-        for which in range(2):
+    pass_on(near, (span_next, span_last, block_next, block_last))
+    for which in range(2):
+        send_in_ring(which, 2)
+    pass_on(far, ((y, lax.rem(z + 2, spans), h), (y, lax.rem(z + spans - 2, spans), h)))
+    for which in range(2):
+        for distance in range(3, spans // 2 + 1):
             send_in_ring(which, distance)
-    for _ in range(blocks // 2):
-        pass_on(block_up, block_next, block_down, block_last)
+    pass_on(across, (block_next, block_last, (lax.rem(y + 2, blocks), z, h)))
 
     for which in range(2):
         for turn in range(blocks):
@@ -183,7 +185,9 @@
             pltpu.SemaphoreType.DMA((2,)),
             pltpu.SemaphoreType.DMA((2,)),
             pltpu.SemaphoreType.DMA((3,)),
-            *[pltpu.SemaphoreType.REGULAR] * 4,
+            pltpu.SemaphoreType.REGULAR((4,)),
+            pltpu.SemaphoreType.REGULAR((2,)),
+            pltpu.SemaphoreType.REGULAR((3,)),
         ],
         compiler_params=pltpu.CompilerParams(
             collective_id=0, has_side_effects=True, vmem_limit_bytes=32 << 20

time: 194 us -> 194 us (level)
  no operation moved by 1% of the time
where the time goes in v5:
time: 194 us
  Pallas kernels  193 us (99%)
    pallas_call x1, Pallas kernels, local(): pl.pallas_call(functools.partial(kernel, blocks, spans, rows), out_shape=...  190 us

profile of v5, /device:TPU:32, one launch (start us, length us, event | category | flops | bytes accessed | tf_op | source)
XLA Modules:
  0.0 193.6 jit_solution(10523532135005316607)
XLA Ops:
  0.6 189.5 %shard_map.58 = (bf16[16384,128]{1,0:T(8,128)(2,1)S(1)}, bf16[16384,128]{1,0:T(8,128)(2,1)S(1)}, f32[1,128]{1,0:T(1,128)S(1)}) custom-call(bf16[16384,128]{1,0:T(8,128)(2,1)} %bitcast.6, bf16[16384,128]{1,0:T(8,128)(2,1)} %bitcast.7, f32[64,16384]{1,0:T(8,128)} %bitcast.8), custom_call_target="tpu_custom_call" | custom-call | tf_op jit(solution)/shard_map/pallas_call | solution.py:172
  190.2 3.4 %shard_map.59 = (bf16[16384,128]{1,0:T(8,128)(2,1)}, bf16[16384,128]{1,0:T(8,128)(2,1)}, f32[1,128]{1,0:T(1,128)}) custom-call(bf16[16384,128]{1,0:T(8,128)(2,1)S(1)} %get-tuple-element.9.keys, bf16[16384,128]{1,0:T(8,128)(2,1)S(1)} %get-tuple-element.10.values, f32[1,128]{1,0:T(1,128)S(1)} %get-tuple-element.11.scale), custom_call_target="tpu_custom_call" | custom-call | tf_op jit(solution)/shard_map/pallas_call | solution.py:205
